TPU v7x, 32 devices: a whole 2x2x4 slice. The times are simulated.
32 devices in a mesh: groups: 2 (over y), pair: 4 (over z), tp: 4 (over x, core).
Axes of the slice: x: 2, y: 2, z: 4, core: 2. Of those that a mesh axis runs over, the one named last changes fastest.
Arguments:
- prompt_keys: bfloat16 [8, 1536, 8, 128], P(('groups', 'pair'), None, 'tp'), parts along dimension 0, may hold values from -6 to 6
- prompt_values: bfloat16 [8, 1536, 8, 128], P(('groups', 'pair'), None, 'tp'), parts along dimension 0, may hold values from -6 to 6
- span_queries: bfloat16 [8, 512, 64, 128], P(('groups', 'pair'), None, 'tp'), parts along dimension 0, may hold values from -1024 to 1024
- span_keys: bfloat16 [8, 512, 8, 128], P(('groups', 'pair'), None, 'tp'), parts along dimension 0, may hold values from -6 to 6
- span_values: bfloat16 [8, 512, 8, 128], P(('groups', 'pair'), None, 'tp'), parts along dimension 0, may hold values from -6 to 6
- prefill_residual: bfloat16 [8, 512, 8192], P(('groups', 'pair'), None, 'tp'), parts along dimension 0, may hold values from -8 to 8
- decode_queries: bfloat16 [8, 2, 32, 64, 128], P(('groups', 'pair'), None, None, 'tp'), parts along dimension 0, may hold values from -1024 to 1024
- decode_keys: bfloat16 [8, 2, 32, 8, 128], P(('groups', 'pair'), None, None, 'tp'), parts along dimension 0, may hold values from -16 to 16
- decode_values: bfloat16 [8, 2, 32, 8, 128], P(('groups', 'pair'), None, None, 'tp'), parts along dimension 0, may hold values from -6 to 6
- decode_residual: bfloat16 [8, 2, 32, 8192], P(('groups', 'pair'), None, None, 'tp'), parts along dimension 0, may hold values from -8 to 8
- cursor: int32 [8, 32], P(('groups', 'pair')), parts along dimension 0, may hold values from 1024 to 2048
- norm_gain: bfloat16 [8192], P('tp'), may hold values from 0.25 to 1.75
Outputs:
- prefill_normed: bfloat16 [8, 512, 8192], P(('groups', 'pair'), None, 'tp'), parts along dimension 0
- handed_keys: bfloat16 [8, 2048, 8, 128], P(('groups', 'pair'), None, 'tp'), parts along dimension 0
- handed_values: bfloat16 [8, 2048, 8, 128], P(('groups', 'pair'), None, 'tp'), parts along dimension 0
- decode_normed: bfloat16 [8, 2, 32, 8192], P(('groups', 'pair'), None, None, 'tp'), parts along dimension 0
There are 2 independent parts, one for each index of `groups`. A program takes and returns all parts, laid end to end along the dimension named above; an argument that names none is the same for every part. Nothing has to cross between parts.
All inputs are finite; a program needn't handle non-finite values.
Results may differ from a plain program's by a relative error of at most 0.0034.
Values may be sent and summed in bfloat16 or wider, within the bound.
A program may use at most 128 MiB of HBM per device.

v0:
```python
import functools

import jax
import jax.numpy as jnp
from jax import lax
from jax.experimental import pallas as pl
from jax.experimental.pallas import tpu as pltpu
from jax.sharding import PartitionSpec as P


epsilon = 1e-05
NT = (((1,), (1,)), ((), ()))
MESH = pl.DeviceIdType.MESH


def from_behind(value, axis, steps):
    count = lax.axis_size(axis)
    pairs = [(source, (source + steps) % count) for source in range(count)]
    return lax.ppermute(value, axis, pairs)


def prefill_kernel(block, past, scale, q_ref, k_ref, v_ref, res_ref, hid_ref, sq_ref):
    span, _ = q_ref.shape[1:]

    @pl.when(pl.program_id(0) == 0)
    def _():
        sq_ref[...] = jnp.zeros_like(sq_ref)

    for start in range(0, span, block):
        rows = slice(start, start + block)
        reach = past + start + block
        scores = lax.dot_general(
            q_ref[0, rows, :], k_ref[0, :reach, :], NT, preferred_element_type=jnp.float32
        )
        row = lax.broadcasted_iota(jnp.int32, (block, block), 0)
        col = lax.broadcasted_iota(jnp.int32, (block, block), 1)
        last = jnp.where(col <= row, scores[:, reach - block :], -jnp.inf)
        scores = jnp.concatenate([scores[:, : reach - block], last], axis=1)
        peak = jnp.max(scores, axis=1, keepdims=True)
        weights = jnp.exp((scores - peak) * scale)
        total = jnp.sum(weights, axis=1, keepdims=True)
        mixed = jnp.dot(
            weights.astype(jnp.bfloat16), v_ref[0, :reach, :], preferred_element_type=jnp.float32
        )
        hidden = mixed / total + res_ref[rows, :].astype(jnp.float32)
        hid_ref[rows, :] = hidden
        sq_ref[rows, :] += hidden * hidden


def prefill(queries, keys, values, residual):
    heads, span, head = queries.shape
    key_heads, positions, _ = keys.shape
    group = heads // key_heads
    block = min(256, span)
    return pl.pallas_call(
        functools.partial(prefill_kernel, block, positions - span, head ** (-0.5)),
        grid=(heads,),
        in_specs=[
            pl.BlockSpec((1, span, head), lambda h: (h, 0, 0)),
            pl.BlockSpec((1, positions, head), lambda h: (h // group, 0, 0)),
            pl.BlockSpec((1, positions, head), lambda h: (h // group, 0, 0)),
            pl.BlockSpec((span, head), lambda h: (0, h)),
        ],
        out_specs=[
            pl.BlockSpec((span, head), lambda h: (0, h)),
            pl.BlockSpec((span, head), lambda h: (0, 0)),
        ],
        out_shape=[
            jax.ShapeDtypeStruct((span, heads * head), jnp.float32),
            jax.ShapeDtypeStruct((span, head), jnp.float32),
        ],
        compiler_params=pltpu.CompilerParams(vmem_limit_bytes=40 * 2**20),
        cost_estimate=pl.CostEstimate(
            flops=8 * heads * span * positions * head,
            bytes_accessed=16 * 2**20,
            transcendentals=heads * span * positions,
        ),
        name="prefill",
    )(queries, keys, values, residual)


def weigh_kernel(
    scale, key_heads, steps, q_ref, pk_ref, sk_ref, dk_ref, dv_ref, cur_ref,
    w_ref, last_ref, inv_ref, own_ref, hk_ref,
):
    g = pl.program_id(0)
    first = jnp.logical_and(g == 0, pl.program_id(1) == 0)
    past = pk_ref.shape[0]

    @pl.when(first)
    def _():
        hk_ref[:past, :] = pk_ref[...]
        hk_ref[past:, :] = sk_ref[...]

    q = q_ref[0]
    rows = q.shape[0]
    scores = jnp.concatenate(
        [
            lax.dot_general(q, pk_ref[...], NT, preferred_element_type=jnp.float32),
            lax.dot_general(q, sk_ref[...], NT, preferred_element_type=jnp.float32),
        ],
        axis=1,
    )
    col = lax.broadcasted_iota(jnp.int32, scores.shape, 1)
    seen = jnp.logical_and(col % key_heads == g, col < cur_ref[...] * key_heads)
    scores = jnp.where(seen, scores, -jnp.inf)
    peak = jnp.max(scores, axis=1, keepdims=True)
    count = dk_ref.shape[2]
    copies = rows // count
    step = lax.broadcasted_iota(jnp.int32, (rows, 1), 0) // count % steps
    wide = q.astype(jnp.float32)
    own_scores = []
    for u in range(steps):
        key = jnp.concatenate([dk_ref[0, u].astype(jnp.float32)] * copies, axis=0)
        own = jnp.sum(wide * key, axis=1, keepdims=True)
        own = jnp.where(step >= u, own, -jnp.inf)
        own_scores.append(own)
        peak = jnp.maximum(peak, own)
    weights = jnp.exp((scores - peak) * scale)
    total = jnp.sum(weights, axis=1, keepdims=True)
    rounded = weights.astype(jnp.bfloat16)
    w_ref[0] = rounded[:, : w_ref.shape[2]]
    last_ref[0] = rounded[:, w_ref.shape[2] :]
    mixed = jnp.zeros(wide.shape, jnp.float32)
    for u in range(steps):
        value = jnp.concatenate([dv_ref[0, u].astype(jnp.float32)] * copies, axis=0)
        weight = jnp.exp((own_scores[u] - peak) * scale)
        total = total + weight
        mixed = mixed + weight.astype(jnp.bfloat16).astype(jnp.float32) * value
    inv_ref[0] = jnp.broadcast_to(1.0 / total, wide.shape)
    own_ref[0] = mixed


def weigh(queries, prompt_keys, span_keys, own_keys, own_values, reach, ending):
    key_heads, rows, head = queries.shape
    _, steps, count, _ = own_keys.shape
    past, span = prompt_keys.shape[0], span_keys.shape[0]
    block = reach.shape[0]
    return pl.pallas_call(
        functools.partial(weigh_kernel, head ** (-0.5), key_heads, steps),
        grid=(key_heads, rows // block),
        in_specs=[
            pl.BlockSpec((1, block, head), lambda g, i: (g, i, 0)),
            pl.BlockSpec((past, head), lambda g, i: (0, 0)),
            pl.BlockSpec((span, head), lambda g, i: (0, 0)),
            pl.BlockSpec((1, steps, count, head), lambda g, i: (g, 0, 0, 0)),
            pl.BlockSpec((1, steps, count, head), lambda g, i: (g, 0, 0, 0)),
            pl.BlockSpec((block, 1), lambda g, i: (0, 0)),
        ],
        out_specs=[
            pl.BlockSpec((1, block, past + span - ending), lambda g, i: (g, i, 0)),
            pl.BlockSpec((1, block, ending), lambda g, i: (g, i, 0)),
            pl.BlockSpec((1, block, head), lambda g, i: (g, i, 0)),
            pl.BlockSpec((1, block, head), lambda g, i: (g, i, 0)),
            pl.BlockSpec((past + span, head), lambda g, i: (0, 0)),
        ],
        out_shape=[
            jax.ShapeDtypeStruct((key_heads, rows, past + span - ending), jnp.bfloat16),
            jax.ShapeDtypeStruct((key_heads, rows, ending), jnp.bfloat16),
            jax.ShapeDtypeStruct((key_heads, rows, head), jnp.float32),
            jax.ShapeDtypeStruct((key_heads, rows, head), jnp.float32),
            jax.ShapeDtypeStruct((past + span, head), jnp.bfloat16),
        ],
        compiler_params=pltpu.CompilerParams(vmem_limit_bytes=40 * 2**20),
        cost_estimate=pl.CostEstimate(
            flops=4 * key_heads * rows * (past + span) * head,
            bytes_accessed=16 * 2**20,
            transcendentals=key_heads * rows * (past + span),
        ),
        name="weigh",
    )(queries, prompt_keys, span_keys, own_keys, own_values, reach)


def mix_kernel(w_ref, v_ref, own_ref, acc_ref, hv_ref):
    @pl.when(pl.program_id(0) == 0)
    def _():
        hv_ref[...] = v_ref[...]

    acc_ref[0] = own_ref[0] + jnp.dot(w_ref[0], v_ref[...], preferred_element_type=jnp.float32)


def mix(weights, prompt_values, own, both):
    key_heads, rows, _ = weights.shape
    past, head = prompt_values.shape
    return pl.pallas_call(
        mix_kernel,
        grid=(key_heads,),
        in_specs=[
            pl.BlockSpec((1, rows, past), lambda g: (g, 0, 0)),
            pl.BlockSpec((past, head), lambda g: (0, 0)),
            pl.BlockSpec((1, rows, head), lambda g: (g, 0, 0)),
        ],
        out_specs=[
            pl.BlockSpec((1, rows, head), lambda g: (g, 0, 0)),
            pl.BlockSpec((past, head), lambda g: (0, 0)),
        ],
        out_shape=[
            jax.ShapeDtypeStruct((key_heads, rows, head), jnp.float32),
            jax.ShapeDtypeStruct((both, head), jnp.bfloat16),
        ],
        compiler_params=pltpu.CompilerParams(vmem_limit_bytes=40 * 2**20),
        cost_estimate=pl.CostEstimate(
            flops=4 * key_heads * rows * past * head, bytes_accessed=8 * 2**20, transcendentals=0
        ),
        name="mix",
    )(weights, prompt_values, own)


def gather_kernel(w_ref, v_ref, acc_ref, inv_ref, res_ref, hv_in, part_ref, hv_ref):
    del hv_in

    @pl.when(pl.program_id(0) == 0)
    def _():
        hv_ref[...] = v_ref[...]

    mixed = acc_ref[0] + jnp.dot(w_ref[0], v_ref[...], preferred_element_type=jnp.float32)
    mixed = mixed * inv_ref[0]
    count = res_ref.shape[0]
    head = mixed.shape[1]
    for h in range(mixed.shape[0] // count):
        columns = slice(h * head, (h + 1) * head)
        part_ref[:, columns] = mixed[h * count : (h + 1) * count] + res_ref[:, columns].astype(jnp.float32)


def gather(weights, span_values, acc, inverse, residual, handed):
    key_heads, rows, _ = weights.shape
    span, head = span_values.shape
    both = handed.shape[0]
    count, width = residual.shape
    at = both // span - 2
    return pl.pallas_call(
        gather_kernel,
        grid=(key_heads,),
        in_specs=[
            pl.BlockSpec((1, rows, span), lambda g: (g, 0, at)),
            pl.BlockSpec((span, head), lambda g: (0, 0)),
            pl.BlockSpec((1, rows, head), lambda g: (g, 0, 0)),
            pl.BlockSpec((1, rows, head), lambda g: (g, 0, 0)),
            pl.BlockSpec((count, width // key_heads), lambda g: (0, g)),
            pl.BlockSpec(memory_space=pl.ANY),
        ],
        out_specs=[
            pl.BlockSpec((count, width // key_heads), lambda g: (0, g)),
            pl.BlockSpec((span, head), lambda g: (at, 0)),
        ],
        out_shape=[
            jax.ShapeDtypeStruct((count, width), jnp.float32),
            jax.ShapeDtypeStruct((both, head), jnp.bfloat16),
        ],
        input_output_aliases={5: 1},
        compiler_params=pltpu.CompilerParams(vmem_limit_bytes=40 * 2**20),
        cost_estimate=pl.CostEstimate(
            flops=4 * key_heads * rows * span * head, bytes_accessed=6 * 2**20, transcendentals=0
        ),
        name="gather",
    )(weights, span_values, acc, inverse, residual, handed)


def close_kernel(
    w_ref, v_ref, part_ref, inv_ref, hid_ref, sum_ref, mine, others, send_sem, recv_sem
):
    devices, me = lax.axis_size("tp"), lax.axis_index("tp")
    ahead = [{"tp": lax.rem(me + k, devices)} for k in range(1, devices)]
    barrier = pltpu.get_barrier_semaphore()
    for peer in ahead:
        pl.semaphore_signal(barrier, inc=1, device_id=peer, device_id_type=MESH)

    key_heads, rows, _ = w_ref.shape
    count = part_ref.shape[0]
    head = v_ref.shape[1]
    squares = jnp.zeros((count, head), jnp.float32)
    for g in range(key_heads):
        mixed = jnp.dot(w_ref[g], v_ref[...], preferred_element_type=jnp.float32) * inv_ref[g]
        for h in range(rows // count):
            at = (g * (rows // count) + h) * head
            hidden = part_ref[:, at : at + head] + mixed[h * count : (h + 1) * count]
            hid_ref[:, at : at + head] = hidden
            squares = squares + hidden * hidden
    sums = jnp.sum(squares, axis=1, keepdims=True)
    lane = lax.broadcasted_iota(jnp.int32, mine.shape, 1)
    tile = jnp.zeros(mine.shape, jnp.float32)
    for k in range(count // mine.shape[0]):
        tile = jnp.where(lane == k, sums[k * mine.shape[0] : (k + 1) * mine.shape[0]], tile)
    mine[...] = tile
    pl.semaphore_wait(barrier, devices - 1)
    copies = [
        pltpu.make_async_remote_copy(
            src_ref=mine,
            dst_ref=others.at[k],
            send_sem=send_sem.at[k],
            recv_sem=recv_sem.at[k],
            device_id=peer,
            device_id_type=MESH,
        )
        for k, peer in enumerate(ahead)
    ]
    for copy in copies:
        copy.start()
    for k, copy in enumerate(copies):
        copy.wait_recv()
        tile = tile + others[k]
    sum_ref[...] = tile
    for copy in copies:
        copy.wait_send()


def close(weights, values, part, inverse):
    count, width = part.shape
    key_heads, rows, span = weights.shape
    head = values.shape[1]
    peers = lax.axis_size("tp") - 1
    vmem = pl.BlockSpec(memory_space=pltpu.VMEM)
    return pl.pallas_call(
        close_kernel,
        in_specs=[vmem] * 4,
        out_specs=[vmem] * 2,
        out_shape=[
            jax.ShapeDtypeStruct((count, width), jnp.float32),
            jax.ShapeDtypeStruct((8, head), jnp.float32),
        ],
        scratch_shapes=[
            pltpu.VMEM((8, head), jnp.float32),
            pltpu.VMEM((peers, 8, head), jnp.float32),
            pltpu.SemaphoreType.DMA((peers,)),
            pltpu.SemaphoreType.DMA((peers,)),
        ],
        compiler_params=pltpu.CompilerParams(
            collective_id=0, has_side_effects=True, vmem_limit_bytes=40 * 2**20
        ),
        cost_estimate=pl.CostEstimate(
            flops=4 * key_heads * rows * span * head, bytes_accessed=4 * 2**20, transcendentals=0
        ),
        name="close",
    )(weights, values, part, inverse)


def write_kernel(
    width, hid_ref, sum_ref, gain_ref, v_ref, hv_in, out_ref, hv_ref, buffer, sems
):
    del hv_in
    span = v_ref.shape[0]
    both = hv_ref.shape[0]
    move = pltpu.make_async_copy(v_ref, hv_ref.at[pl.ds(both - span, span)], sems.at[0])
    move.start()
    scale = lax.rsqrt(sum_ref[...] / width + epsilon)
    tall = scale.shape[0]
    moves = [move]
    step = 2 * tall
    for n, start in enumerate(range(0, hid_ref.shape[0], step)):
        rows = slice(start, start + step)
        first = start // tall
        each = jnp.concatenate([scale[:, first + k : first + k + 1] for k in range(2)], axis=0)
        buffer[rows, :] = (hid_ref[rows, :] * each * gain_ref[...]).astype(jnp.bfloat16)
        out = pltpu.make_async_copy(buffer.at[pl.ds(start, step)], out_ref.at[pl.ds(start, step)], sems.at[n + 1])
        out.start()
        moves.append(out)
    for move in moves:
        move.wait()


def write(hidden, sums, gain, values, handed):
    count, columns = hidden.shape
    vmem = pl.BlockSpec(memory_space=pltpu.VMEM)
    anywhere = pl.BlockSpec(memory_space=pl.ANY)
    return pl.pallas_call(
        functools.partial(write_kernel, columns * lax.axis_size("tp")),
        in_specs=[vmem] * 4 + [anywhere],
        out_specs=[anywhere] * 2,
        out_shape=[
            jax.ShapeDtypeStruct((count, columns), jnp.bfloat16),
            jax.ShapeDtypeStruct(handed.shape, jnp.bfloat16),
        ],
        scratch_shapes=[
            pltpu.VMEM((count, columns), jnp.bfloat16),
            pltpu.SemaphoreType.DMA((1 + count // 16,)),
        ],
        input_output_aliases={4: 1},
        compiler_params=pltpu.CompilerParams(vmem_limit_bytes=40 * 2**20),
        cost_estimate=pl.CostEstimate(
            flops=8 * count * columns, bytes_accessed=2 * 2**20, transcendentals=0
        ),
        name="write",
    )(hidden, sums, gain, values, handed)


def normed(hidden, partial, gain):
    width = hidden.shape[1] * lax.axis_size("tp")
    squares = lax.psum(jnp.sum(partial, axis=1), "tp")
    scaled = hidden * lax.rsqrt(squares[:, None] / width + epsilon) * gain.astype(jnp.float32)
    return scaled.astype(jnp.bfloat16)


def local(
    prompt_keys,
    prompt_values,
    span_queries,
    span_keys,
    span_values,
    prefill_residual,
    decode_queries,
    decode_keys,
    decode_values,
    decode_residual,
    cursor,
    norm_gain,
):
    halfway = lax.axis_size("pair") // 2
    span, heads, head = span_queries.shape[1:]
    past, key_heads = prompt_keys.shape[1:3]
    steps, count = decode_keys.shape[1:3]
    group = heads // key_heads
    flat = lambda a: a.reshape(-1, head)
    far = []
    early = span // 2
    pieces = (prompt_keys, span_keys, prompt_values, span_values[:, :early], span_values[:, early:])
    for piece in pieces:
        far.append(from_behind(flat(piece), "pair", halfway))
    far_pk, far_sk, far_pv, far_sv, far_tv = far

    keys = jnp.concatenate([prompt_keys[0], span_keys[0]], axis=0).transpose(1, 0, 2)
    values = jnp.concatenate([prompt_values[0], span_values[0]], axis=0).transpose(1, 0, 2)
    queries = span_queries[0].transpose(1, 0, 2)
    prefill_hidden, prefill_partial = prefill(queries, keys, values, prefill_residual[0])
    prefill_out = normed(prefill_hidden, prefill_partial, norm_gain)

    dq = decode_queries[0].reshape(steps * count, heads, head).transpose(1, 0, 2)
    dq = dq.reshape(key_heads, group * steps * count, head)
    dk = decode_keys[0].transpose(2, 0, 1, 3)
    dv = decode_values[0].transpose(2, 0, 1, 3)
    block = steps * count * (2 if group % 2 == 0 else 1)
    reach = jnp.tile(cursor[0], block // count)[:, None]
    prefill_out, dq, dk, dv, reach = lax.optimization_barrier((prefill_out, dq, dk, dv, reach))
    weights, ending, inverse, own, handed_keys = weigh(
        dq, far_pk, far_sk, dk, dv, reach, far_tv.shape[0]
    )
    acc, handed = mix(weights, far_pv, own, (past + span) * key_heads)
    residual = decode_residual[0].reshape(steps * count, heads * head)
    part, handed = gather(weights, far_sv, acc, inverse, residual, handed)
    decode_hidden, sums = close(ending, far_tv, part, inverse)
    gain = norm_gain.astype(jnp.float32)[None, :]
    decode_out, handed_values = write(decode_hidden, sums, gain, far_tv, handed)
    shape = (1, past + span, key_heads, head)
    return (
        prefill_out[None],
        handed_keys.reshape(shape),
        handed_values.reshape(shape),
        decode_out.reshape(decode_residual.shape),
    )


def solution(mesh):
    row = ("groups", "pair")
    placed = (
        P(row, None, "tp", None),
        P(row, None, "tp", None),
        P(row, None, "tp", None),
        P(row, None, "tp", None),
        P(row, None, "tp", None),
        P(row, None, "tp"),
        P(row, None, None, "tp", None),
        P(row, None, None, "tp", None),
        P(row, None, None, "tp", None),
        P(row, None, None, "tp"),
        P(row, None),
        P("tp"),
    )
    return jax.shard_map(
        local,
        mesh=mesh,
        in_specs=placed,
        out_specs=(
            P(row, None, "tp"),
            P(row, None, "tp", None),
            P(row, None, "tp", None),
            P(row, None, None, "tp"),
        ),
        check_vma=False,
    )
```

profile of v0, /device:TPU:0, one launch (start us, length us, event | category | flops | bytes accessed | tf_op | source)
XLA Modules:
  0.0 117.5 jit_solution(3450093573571797634)
XLA Ops:
  0.6 0.0 copy-start.5
  0.6 0.0 copy-start.4
  0.7 1.3 %fusion = (bf16[1,256,2,128]{3,2,1,0:T(2,128)(2,1)S(1)}, bf16[1,256,2,128]{3,2,1,0:T(2,128)(2,1)S(1)}) fusion(bf16[1,512,2,128]{3,2,1,0:T(2,128)(2,1)} %param.16), kind=kLoop, calls=%fused_computation.11 | loop fusion | bytes 524288 | tf_op jit(solution)/shard_map/slice | solution.py:415
  1.9 4.1 %collective-permute-start.2 = (bf16[512,128]{1,0:T(8,128)(2,1)S(1)}, bf16[512,128]{1,0:T(8,128)(2,1)S(1)}, u32[]{:S(2)}, u32[]{:S(2)}) collective-permute-start(bf16[512,128]{1,0:T(8,128)(2,1)S(1)} %bitcast.61), channel_id=1, source_target_pairs={{0,8},{4,12},{8,0},{12,4},{1,9},{5,13},{9,1},{13,5},{2,10},{6,14},... | collective-permute-start | bytes 393224 | tf_op jit(solution)/shard_map/ppermute | solution.py:19
  6.1 0.1 collective-permute-start.3
  6.1 2.8 %collective-permute-start.1 = (bf16[1024,128]{1,0:T(8,128)(2,1)}, bf16[1024,128]{1,0:T(8,128)(2,1)S(1)}, u32[]{:S(2)}, u32[]{:S(2)}) collective-permute-start(bf16[1024,128]{1,0:T(8,128)(2,1)} %bitcast.60), channel_id=1, source_target_pairs={{0,8},{4,12},{8,0},{12,4},{1,9},{5,13},{9,1},{13,5},{2,10},{6,14},... | collective-permute-start | bytes 786440 | tf_op jit(solution)/shard_map/ppermute | solution.py:19
  9.0 0.1 collective-permute-start.4
  9.1 0.0 copy-start.9
  9.1 2.8 %collective-permute-start = (bf16[3072,128]{1,0:T(8,128)(2,1)}, bf16[3072,128]{1,0:T(8,128)(2,1)S(1)}, u32[]{:S(2)}, u32[]{:S(2)}) collective-permute-start(bf16[3072,128]{1,0:T(8,128)(2,1)} %bitcast.57), channel_id=1, source_target_pairs={{0,8},{4,12},{8,0},{12,4},{1,9},{5,13},{9,1},{13,5},{2,10},{6,14},... | collective-permute-start | bytes 2359304 | tf_op jit(solution)/shard_map/ppermute | solution.py:19
  11.9 1.0 copy.38
  12.9 1.0 copy.37
  13.9 0.0 copy-done.4
  13.9 0.1 copy.36
  14.0 0.0 copy-done.5
  14.0 0.1 copy.35
  14.1 0.0 copy-done.9
  14.2 0.0 copy-done.3
  14.2 0.5 copy.34
  14.7 0.0 copy-start.2
  14.7 0.1 maximum_bitcast_fusion.k_ref
  14.8 0.1 maximum_bitcast_fusion.1.v_ref
  14.9 1.4 %copy-done.2 = bf16[1,512,2048]{2,1,0:T(8,128)(2,1)S(1)} copy-done((bf16[1,512,2048]{2,1,0:T(8,128)(2,1)S(1)}, bf16[1,512,2048]{2,1,0:T(8,128)(2,1)}, u32[]{:S(2)}) %copy-start.2) | copy-done | bytes 2097176
  16.3 32.3 %prefill.1 = (f32[512,2048]{1,0:T(8,128)S(1)}, f32[512,128]{1,0:T(8,128)S(1)}) custom-call(bf16[16,512,128]{2,1,0:T(8,128)(2,1)S(1)} %bitcast.46, bf16[2,2048,128]{2,1,0:T(8,128)(2,1)S(1)} %maximum_bitcast_fusion.k_ref, bf16[2,2048,128]{2,1,0:T(8,128)(2,1)S(1)} %maximum_bitcast_fusion.1.v_ref, bf16[512,2048]{1,0:T(8,128)(2,1)S(1)} %bitcast.50), custom_call_target="tpu_custom_call" | custom-call | flops 17179869184 | bytes 16777216 | tf_op jit(solution)/shard_map/prefill/pallas_call | solution.py:55
  48.6 0.0 copy-start
  48.6 1.9 %copy-done = f32[512,2048]{1,0:T(8,128)} copy-done((f32[512,2048]{1,0:T(8,128)}, f32[512,2048]{1,0:T(8,128)S(1)}, u32[]{:S(2)}) %copy-start) | copy-done | bytes 4194328
  50.6 0.1 reduce_sum.9
  50.7 6.0 %psum.7 = f32[512]{0:T(512)S(1)} all-reduce(f32[512]{0:T(512)S(1)} %reduce_sum.9), channel_id=1, replica_groups=mesh['groups'=2,'pair'=4,'tp'=4] {'tp'}, use_global_device_ids=true, to_apply=%region_1.0 | all-reduce | flops 512 | bytes 4096 | tf_op jit(solution)/shard_map/psum | solution.py:388
  56.7 0.0 copy-start.7
  56.7 0.0 copy-start.8
  56.7 4.0 %multiply_convert_fusion = bf16[512,2048]{1,0:T(8,128)(2,1)} fusion(f32[512,2048]{1,0:T(8,128)} %copy-done, f32[2048]{0:T(1024)S(1)} %convert_element_type.7, f32[512]{0:T(512)S(1)} %add_rsqrt_fusion), kind=kLoop, calls=%fused_computation | loop fusion | flops 3145728 | bytes 6301696 | tf_op jit(solution)/shard_map/convert_element_type | solution.py:390
  60.7 0.0 copy-done.10
  60.7 0.1 broadcast_in_dim_tile.3
  60.8 0.0 copy-done.6
  60.8 0.1 copy.23
  60.9 0.0 copy-done.7
  60.9 0.0 copy-done.8
  60.9 0.1 copy.26.cur_ref
  61.0 2.8 %collective-permute-done.1.sk_ref = bf16[1024,128]{1,0:T(8,128)(2,1)S(1)} collective-permute-done((bf16[1024,128]{1,0:T(8,128)(2,1)}, bf16[1024,128]{1,0:T(8,128)(2,1)S(1)}, u32[]{:S(2)}, u32[]{:S(2)}) %collective-permute-start.1) | collective-permute-done | bytes 262176 | tf_op jit(solution)/shard_map/ppermute | solution.py:19
  63.8 32.9 %collective-permute-done.pk_ref = bf16[3072,128]{1,0:T(8,128)(2,1)S(1)} collective-permute-done((bf16[3072,128]{1,0:T(8,128)(2,1)}, bf16[3072,128]{1,0:T(8,128)(2,1)S(1)}, u32[]{:S(2)}, u32[]{:S(2)}) %collective-permute-start) | collective-permute-done | bytes 786464 | tf_op jit(solution)/shard_map/ppermute | solution.py:19
  96.6 11.6 %weigh.1 = (bf16[2,512,3584]{2,1,0:T(8,128)(2,1)S(1)}, bf16[2,512,512]{2,1,0:T(8,128)(2,1)S(1)}, f32[2,512,128]{2,1,0:T(8,128)S(1)}, f32[2,512,128]{2,1,0:T(8,128)S(1)}, bf16[4096,128]{1,0:T(8,128)(2,1)}) custom-call(bf16[2,512,128]{2,1,0:T(8,128)(2,1)S(1)} %bitcast.48, bf16[3072,128]{1,0:T(8,128)(2,1)S(1)} %collective-permute-done.pk_ref, ...), custom_call_target="tpu_custom_call" | custom-call | flops 2147483648 | bytes 16777216 | tf_op jit(solution)/shard_map/weigh/pallas_call | solution.py:139
  108.2 0.0 collective-permute-done.4.v_ref
  108.3 3.2 %mix.1 = (f32[2,512,128]{2,1,0:T(8,128)S(1)}, bf16[4096,128]{1,0:T(8,128)(2,1)}) custom-call(bf16[2,512,3584]{2,1,0:T(8,128)(2,1)S(1)} %get-tuple-element.33.w_ref, bf16[3072,128]{1,0:T(8,128)(2,1)S(1)} %collective-permute-done.4.v_ref, f32[2,512,128]{2,1,0:T(8,128)S(1)} %get-tuple-element.34.own_ref), custom_call_target="tpu_custom_call" | custom-call | flops 1610612736 | bytes 8388608 | tf_op jit(solution)/shard_map/mix/pallas_call | solution.py:185
  111.5 0.0 collective-permute-done.3.v_ref
  111.5 0.0 copy-done.1
  111.5 1.4 %gather.1 = (f32[64,2048]{1,0:T(8,128)S(1)}, bf16[4096,128]{1,0:T(8,128)(2,1)}) custom-call(bf16[2,512,3584]{2,1,0:T(8,128)(2,1)S(1)} %get-tuple-element.33.w_ref, bf16[512,128]{1,0:T(8,128)(2,1)S(1)} %collective-permute-done.3.v_ref, f32[2,512,128]{2,1,0:T(8,128)S(1)} %get-tuple-element.35.acc_ref, ...), custom_call_target="tpu_custom_call", output_to_operand_aliasing={{1}: (5, {})} | custom-call | flops 268435456 | bytes 6291456 | tf_op jit(solution)/shard_map/gather/pallas_call | solution.py:231
  112.9 0.0 collective-permute-done.2.v_ref
  112.9 3.7 %close.1 = (f32[64,2048]{1,0:T(8,128)S(1)}, f32[8,128]{1,0:T(8,128)S(1)}) custom-call(bf16[2,512,512]{2,1,0:T(8,128)(2,1)S(1)} %get-tuple-element.32.w_ref, bf16[512,128]{1,0:T(8,128)(2,1)S(1)} %collective-permute-done.2.v_ref, f32[64,2048]{1,0:T(8,128)S(1)} %get-tuple-element.38.part_ref, f32[2,512,128]{2,1,0:T(8,128)S(1)} %get-tuple-element.36.inv_ref), custom_call_target="tpu_custom_call" | custom-call | flops 268435456 | bytes 4194304 | tf_op jit(solution)/shard_map/close/pallas_call | solution.py:313
  116.6 0.9 write.1
  (8 shorter events, 0.0 us)
Async XLA Ops:
  0.6 13.4 %copy-start.5 = (bf16[1,1536,2,128]{3,2,1,0:T(2,128)(2,1)S(1)}, bf16[1,1536,2,128]{3,2,1,0:T(2,128)(2,1)}, u32[]{:S(2)}) copy-start(bf16[1,1536,2,128]{3,2,1,0:T(2,128)(2,1)} %param.13) | copy-start | bytes 2359300
  0.6 13.2 %copy-start.4 = (bf16[1,1536,2,128]{3,2,1,0:T(2,128)(2,1)S(1)}, bf16[1,1536,2,128]{3,2,1,0:T(2,128)(2,1)}, u32[]{:S(2)}) copy-start(bf16[1,1536,2,128]{3,2,1,0:T(2,128)(2,1)} %param.12) | copy-start | bytes 2359300
  1.9 111.0 %collective-permute-start.2 = (bf16[512,128]{1,0:T(8,128)(2,1)S(1)}, bf16[512,128]{1,0:T(8,128)(2,1)S(1)}, u32[]{:S(2)}, u32[]{:S(2)}) collective-permute-start(bf16[512,128]{1,0:T(8,128)(2,1)S(1)} %bitcast.61), channel_id=1, source_target_pairs={{0,8},{4,12},{8,0},{12,4},{1,9},{5,13},{9,1},{13,5},{2,10},{6,14},... | collective-permute-start | bytes 393224 | tf_op jit(solution)/shard_map/ppermute | solution.py:19
  6.1 105.4 %collective-permute-start.3 = (bf16[512,128]{1,0:T(8,128)(2,1)S(1)}, bf16[512,128]{1,0:T(8,128)(2,1)S(1)}, u32[]{:S(2)}, u32[]{:S(2)}) collective-permute-start(bf16[512,128]{1,0:T(8,128)(2,1)S(1)} %bitcast.62), channel_id=1, source_target_pairs={{0,8},{4,12},{8,0},{12,4},{1,9},{5,13},{9,1},{13,5},{2,10},{6,14},... | collective-permute-start | bytes 393224 | tf_op jit(solution)/shard_map/ppermute | solution.py:19
  6.1 57.6 %collective-permute-start.1 = (bf16[1024,128]{1,0:T(8,128)(2,1)}, bf16[1024,128]{1,0:T(8,128)(2,1)S(1)}, u32[]{:S(2)}, u32[]{:S(2)}) collective-permute-start(bf16[1024,128]{1,0:T(8,128)(2,1)} %bitcast.60), channel_id=1, source_target_pairs={{0,8},{4,12},{8,0},{12,4},{1,9},{5,13},{9,1},{13,5},{2,10},{6,14},... | collective-permute-start | bytes 786440 | tf_op jit(solution)/shard_map/ppermute | solution.py:19
  9.0 99.3 %collective-permute-start.4 = (bf16[3072,128]{1,0:T(8,128)(2,1)}, bf16[3072,128]{1,0:T(8,128)(2,1)S(1)}, u32[]{:S(2)}, u32[]{:S(2)}) collective-permute-start(bf16[3072,128]{1,0:T(8,128)(2,1)} %bitcast.58), channel_id=1, source_target_pairs={{0,8},{4,12},{8,0},{12,4},{1,9},{5,13},{9,1},{13,5},{2,10},{6,14},... | collective-permute-start | bytes 2359304 | tf_op jit(solution)/shard_map/ppermute | solution.py:19
  9.1 5.1 %copy-start.9 = (bf16[2048]{0:T(1024)(128)(2,1)S(1)}, bf16[2048]{0:T(1024)(128)(2,1)}, u32[]{:S(2)}) copy-start(bf16[2048]{0:T(1024)(128)(2,1)} %param.23) | copy-start | bytes 12292
  9.1 5.1 %copy-start.3 = (bf16[1,512,16,128]{3,2,1,0:T(8,128)(2,1)S(1)}, bf16[1,512,16,128]{3,2,1,0:T(8,128)(2,1)}, u32[]{:S(2)}) copy-start(bf16[1,512,16,128]{3,2,1,0:T(8,128)(2,1)} %param.14) | copy-start | bytes 6291460
  9.1 87.6 %collective-permute-start = (bf16[3072,128]{1,0:T(8,128)(2,1)}, bf16[3072,128]{1,0:T(8,128)(2,1)S(1)}, u32[]{:S(2)}, u32[]{:S(2)}) collective-permute-start(bf16[3072,128]{1,0:T(8,128)(2,1)} %bitcast.57), channel_id=1, source_target_pairs={{0,8},{4,12},{8,0},{12,4},{1,9},{5,13},{9,1},{13,5},{2,10},{6,14},... | collective-permute-start | bytes 2359304 | tf_op jit(solution)/shard_map/ppermute | solution.py:19
  14.7 1.6 %copy-start.2 = (bf16[1,512,2048]{2,1,0:T(8,128)(2,1)S(1)}, bf16[1,512,2048]{2,1,0:T(8,128)(2,1)}, u32[]{:S(2)}) copy-start(bf16[1,512,2048]{2,1,0:T(8,128)(2,1)} %param.17) | copy-start | bytes 6291460
  48.6 2.0 %copy-start = (f32[512,2048]{1,0:T(8,128)}, f32[512,2048]{1,0:T(8,128)S(1)}, u32[]{:S(2)}) copy-start(f32[512,2048]{1,0:T(8,128)S(1)} %get-tuple-element.24) | copy-start | bytes 12582916
  56.7 4.0 %copy-start.10 = (s32[1,32]{1,0:T(1,128)S(1)}, s32[1,32]{1,0:T(1,128)}, u32[]{:S(2)}) copy-start(s32[1,32]{1,0:T(1,128)} %param.22) | copy-start | bytes 388
  56.7 4.1 %copy-start.6 = (bf16[1,2,32,16,128]{4,3,2,1,0:T(8,128)(2,1)S(1)}, bf16[1,2,32,16,128]{4,3,2,1,0:T(8,128)(2,1)}, u32[]{:S(2)}) copy-start(bf16[1,2,32,16,128]{4,3,2,1,0:T(8,128)(2,1)} %param.18) | copy-start | bytes 786436
  56.7 4.2 %copy-start.7 = (bf16[1,2,32,2,128]{4,3,2,1,0:T(2,128)(2,1)S(1)}, bf16[1,2,32,2,128]{4,3,2,1,0:T(2,128)(2,1)}, u32[]{:S(2)}) copy-start(bf16[1,2,32,2,128]{4,3,2,1,0:T(2,128)(2,1)} %param.20) | copy-start | bytes 98308
  56.7 4.1 %copy-start.8 = (bf16[1,2,32,2,128]{4,3,2,1,0:T(2,128)(2,1)S(1)}, bf16[1,2,32,2,128]{4,3,2,1,0:T(2,128)(2,1)}, u32[]{:S(2)}) copy-start(bf16[1,2,32,2,128]{4,3,2,1,0:T(2,128)(2,1)} %param.19) | copy-start | bytes 98308
  108.3 3.2 %copy-start.1 = (bf16[1,2,32,2048]{3,2,1,0:T(8,128)(2,1)S(1)}, bf16[1,2,32,2048]{3,2,1,0:T(8,128)(2,1)}, u32[]{:S(2)}) copy-start(bf16[1,2,32,2048]{3,2,1,0:T(8,128)(2,1)} %param.21) | copy-start | bytes 786436
where the time goes:
time: 118 us
  Pallas kernels  53.2 us (45%)
  waiting for transfers between devices  35.6 us (30%)
  starting transfers between devices  9.98 us (8%)
  local copies, waits for them, and re-layouts  7.69 us (7%)
  blocking collectives  5.96 us (5%)
  other arithmetic  4.25 us (4%)
    ppermute x5, waiting for transfers between devices, from_behind(): return lax.ppermute(value, axis, pairs)  35.6 us
    pallas_call x1, Pallas kernels, prefill(): pl.pallas_call(functools.partial(prefill_kernel, block, positions - span,...  32.3 us
    pallas_call x1, Pallas kernels, weigh(): pl.pallas_call(functools.partial(weigh_kernel, head ** (-0.5), key_heads,...  11.6 us
    ppermute x5, starting transfers between devices, from_behind(): return lax.ppermute(value, axis, pairs)  9.98 us
    unnamed x27, local copies, waits for them, and re-layouts  6.15 us
    psum x1, blocking collectives, normed(): squares = lax.psum(jnp.sum(partial, axis=1), 'tp')  5.96 us
    convert_element_type x1, other arithmetic, normed(): return scaled.astype(jnp.bfloat16)  3.96 us
    pallas_call x1, Pallas kernels, close(): pl.pallas_call(close_kernel, in_specs=[vmem] * 4, out_specs=[vmem] * 2, o...  3.72 us
  transfers between devices with their start and end apart: 5, of which 2 were waited for; matrix products, arithmetic and copies ran while one was open for 6% of the time, Pallas kernels for 41%

commit v1 on v0

--- a/solution.py
+++ b/solution.py
@@ -206,13 +206,42 @@
     )(weights, prompt_values, own)
 
 
-def gather_kernel(w_ref, v_ref, acc_ref, inv_ref, res_ref, hv_in, part_ref, hv_ref):
+def mix_more_kernel(w_ref, v_ref, own_ref, hv_in, acc_ref, hv_ref):
     del hv_in
-
-    @pl.when(pl.program_id(0) == 0)
-    def _():
-        hv_ref[...] = v_ref[...]
-
+    mix_kernel(w_ref, v_ref, own_ref, acc_ref, hv_ref)
+
+
+def mix_more(weights, values, acc, handed, start):
+    key_heads, rows, _ = weights.shape
+    span, head = values.shape
+    at = start // span
+    return pl.pallas_call(
+        mix_more_kernel,
+        grid=(key_heads,),
+        in_specs=[
+            pl.BlockSpec((1, rows, span), lambda g: (g, 0, at)),
+            pl.BlockSpec((span, head), lambda g: (0, 0)),
+            pl.BlockSpec((1, rows, head), lambda g: (g, 0, 0)),
+            pl.BlockSpec(memory_space=pl.ANY),
+        ],
+        out_specs=[
+            pl.BlockSpec((1, rows, head), lambda g: (g, 0, 0)),
+            pl.BlockSpec((span, head), lambda g: (at, 0)),
+        ],
+        out_shape=[
+            jax.ShapeDtypeStruct((key_heads, rows, head), jnp.float32),
+            jax.ShapeDtypeStruct(handed.shape, jnp.bfloat16),
+        ],
+        input_output_aliases={3: 1},
+        compiler_params=pltpu.CompilerParams(vmem_limit_bytes=40 * 2**20),
+        cost_estimate=pl.CostEstimate(
+            flops=4 * key_heads * rows * span * head, bytes_accessed=6 * 2**20, transcendentals=0
+        ),
+        name="mix_more",
+    )(weights, values, acc, handed)
+
+
+def gather_kernel(w_ref, v_ref, acc_ref, inv_ref, res_ref, part_ref):
     mixed = acc_ref[0] + jnp.dot(w_ref[0], v_ref[...], preferred_element_type=jnp.float32)
     mixed = mixed * inv_ref[0]
     count = res_ref.shape[0]
@@ -222,12 +251,11 @@
         part_ref[:, columns] = mixed[h * count : (h + 1) * count] + res_ref[:, columns].astype(jnp.float32)
 
 
-def gather(weights, span_values, acc, inverse, residual, handed):
-    key_heads, rows, _ = weights.shape
+def gather(weights, span_values, acc, inverse, residual):
+    key_heads, rows, columns = weights.shape
     span, head = span_values.shape
-    both = handed.shape[0]
     count, width = residual.shape
-    at = both // span - 2
+    at = columns // span - 1
     return pl.pallas_call(
         gather_kernel,
         grid=(key_heads,),
@@ -237,23 +265,15 @@
             pl.BlockSpec((1, rows, head), lambda g: (g, 0, 0)),
             pl.BlockSpec((1, rows, head), lambda g: (g, 0, 0)),
             pl.BlockSpec((count, width // key_heads), lambda g: (0, g)),
-            pl.BlockSpec(memory_space=pl.ANY),
-        ],
-        out_specs=[
-            pl.BlockSpec((count, width // key_heads), lambda g: (0, g)),
-            pl.BlockSpec((span, head), lambda g: (at, 0)),
-        ],
-        out_shape=[
-            jax.ShapeDtypeStruct((count, width), jnp.float32),
-            jax.ShapeDtypeStruct((both, head), jnp.bfloat16),
-        ],
-        input_output_aliases={5: 1},
+        ],
+        out_specs=pl.BlockSpec((count, width // key_heads), lambda g: (0, g)),
+        out_shape=jax.ShapeDtypeStruct((count, width), jnp.float32),
         compiler_params=pltpu.CompilerParams(vmem_limit_bytes=40 * 2**20),
         cost_estimate=pl.CostEstimate(
             flops=4 * key_heads * rows * span * head, bytes_accessed=6 * 2**20, transcendentals=0
         ),
         name="gather",
-    )(weights, span_values, acc, inverse, residual, handed)
+    )(weights, span_values, acc, inverse, residual)
 
 
 def close_kernel(
@@ -335,36 +355,42 @@
 
 
 def write_kernel(
-    width, hid_ref, sum_ref, gain_ref, v_ref, hv_in, out_ref, hv_ref, buffer, sems
+    width, hid_ref, sum_ref, gain_ref, s_ref, t_ref, hv_in, out_ref, hv_ref, buffer, sems
 ):
     del hv_in
-    span = v_ref.shape[0]
-    both = hv_ref.shape[0]
-    move = pltpu.make_async_copy(v_ref, hv_ref.at[pl.ds(both - span, span)], sems.at[0])
-    move.start()
+    ends = hv_ref.shape[0]
+    moves = []
+    for v_ref in (t_ref, s_ref):
+        ends -= v_ref.shape[0]
+        moves.append(
+            pltpu.make_async_copy(v_ref, hv_ref.at[pl.ds(ends, v_ref.shape[0])], sems.at[len(moves)])
+        )
+        moves[-1].start()
     scale = lax.rsqrt(sum_ref[...] / width + epsilon)
     tall = scale.shape[0]
-    moves = [move]
     step = 2 * tall
-    for n, start in enumerate(range(0, hid_ref.shape[0], step)):
+    for start in range(0, hid_ref.shape[0], step):
         rows = slice(start, start + step)
         first = start // tall
         each = jnp.concatenate([scale[:, first + k : first + k + 1] for k in range(2)], axis=0)
         buffer[rows, :] = (hid_ref[rows, :] * each * gain_ref[...]).astype(jnp.bfloat16)
-        out = pltpu.make_async_copy(buffer.at[pl.ds(start, step)], out_ref.at[pl.ds(start, step)], sems.at[n + 1])
-        out.start()
-        moves.append(out)
+        moves.append(
+            pltpu.make_async_copy(
+                buffer.at[pl.ds(start, step)], out_ref.at[pl.ds(start, step)], sems.at[len(moves)]
+            )
+        )
+        moves[-1].start()
     for move in moves:
         move.wait()
 
 
-def write(hidden, sums, gain, values, handed):
+def write(hidden, sums, gain, values, last_values, handed):
     count, columns = hidden.shape
     vmem = pl.BlockSpec(memory_space=pltpu.VMEM)
     anywhere = pl.BlockSpec(memory_space=pl.ANY)
     return pl.pallas_call(
         functools.partial(write_kernel, columns * lax.axis_size("tp")),
-        in_specs=[vmem] * 4 + [anywhere],
+        in_specs=[vmem] * 5 + [anywhere],
         out_specs=[anywhere] * 2,
         out_shape=[
             jax.ShapeDtypeStruct((count, columns), jnp.bfloat16),
@@ -372,15 +398,15 @@
         ],
         scratch_shapes=[
             pltpu.VMEM((count, columns), jnp.bfloat16),
-            pltpu.SemaphoreType.DMA((1 + count // 16,)),
-        ],
-        input_output_aliases={4: 1},
+            pltpu.SemaphoreType.DMA((2 + count // 16,)),
+        ],
+        input_output_aliases={5: 1},
         compiler_params=pltpu.CompilerParams(vmem_limit_bytes=40 * 2**20),
         cost_estimate=pl.CostEstimate(
             flops=8 * count * columns, bytes_accessed=2 * 2**20, transcendentals=0
         ),
         name="write",
-    )(hidden, sums, gain, values, handed)
+    )(hidden, sums, gain, values, last_values, handed)
 
 
 def normed(hidden, partial, gain):
@@ -411,11 +437,18 @@
     group = heads // key_heads
     flat = lambda a: a.reshape(-1, head)
     far = []
-    early = span // 2
-    pieces = (prompt_keys, span_keys, prompt_values, span_values[:, :early], span_values[:, early:])
+    early, most = span // 2, past - past // 3
+    pieces = (
+        prompt_keys,
+        span_keys,
+        prompt_values[:, :most],
+        prompt_values[:, most:],
+        span_values[:, :early],
+        span_values[:, early:],
+    )
     for piece in pieces:
         far.append(from_behind(flat(piece), "pair", halfway))
-    far_pk, far_sk, far_pv, far_sv, far_tv = far
+    far_pk, far_sk, far_pv, far_qv, far_sv, far_tv = far
 
     keys = jnp.concatenate([prompt_keys[0], span_keys[0]], axis=0).transpose(1, 0, 2)
     values = jnp.concatenate([prompt_values[0], span_values[0]], axis=0).transpose(1, 0, 2)
@@ -434,11 +467,12 @@
         dq, far_pk, far_sk, dk, dv, reach, far_tv.shape[0]
     )
     acc, handed = mix(weights, far_pv, own, (past + span) * key_heads)
+    acc, handed = mix_more(weights, far_qv, acc, handed, most * key_heads)
     residual = decode_residual[0].reshape(steps * count, heads * head)
-    part, handed = gather(weights, far_sv, acc, inverse, residual, handed)
+    part = gather(weights, far_sv, acc, inverse, residual)
     decode_hidden, sums = close(ending, far_tv, part, inverse)
     gain = norm_gain.astype(jnp.float32)[None, :]
-    decode_out, handed_values = write(decode_hidden, sums, gain, far_tv, handed)
+    decode_out, handed_values = write(decode_hidden, sums, gain, far_sv, far_tv, handed)
     shape = (1, past + span, key_heads, head)
     return (
         prefill_out[None],

time: 118 us -> 100 us (0.85)
  waiting for transfers between devices: 35.6 us -> 15.4 us
  local copies, waits for them, and re-layouts: 7.69 us -> 10.4 us
    ppermute x5 -> x6, waiting for transfers between devices: 35.6 us -> 15.4 us  [from_behind(): return lax.ppermute(value, axis, pairs)]
    slice x0 -> x2, local copies, waits for them, and re-layouts: none -> 4.08 us  [the longest x1 2.25 us: local(): prompt_values[:, :most]]
    unnamed x27 -> x31, local copies, waits for them, and re-layouts: 6.15 us -> 4.24 us
    pallas_call x0 -> x1, Pallas kernels: none -> 1.64 us  [mix_more(): pl.pallas_call(mix_more_kernel, grid=(key_heads,), in_specs=[pl.BlockSpec...]
    ppermute x5 -> x6, starting transfers between devices: 9.98 us -> 9.93 us  [from_behind(): return lax.ppermute(value, axis, pairs)]
  transfers between devices with their start and end apart: 5 -> 6, of which waited for: 2 -> 5; matrix products, arithmetic and copies ran while one was open for 6% -> 11% of each run, Pallas kernels for 41% -> 49%
where the time goes in v1:
time: 100 us
  Pallas kernels  53.4 us (53%)
  waiting for transfers between devices  15.4 us (15%)
  local copies, waits for them, and re-layouts  10.4 us (10%)
  starting transfers between devices  9.93 us (10%)
  blocking collectives  5.96 us (6%)
  other arithmetic  4.24 us (4%)
    pallas_call x1, Pallas kernels, prefill(): pl.pallas_call(functools.partial(prefill_kernel, block, positions - span,...  32.3 us
    ppermute x6, waiting for transfers between devices, from_behind(): return lax.ppermute(value, axis, pairs)  15.4 us
    pallas_call x1, Pallas kernels, weigh(): pl.pallas_call(functools.partial(weigh_kernel, head ** (-0.5), key_heads,...  11.6 us
    ppermute x6, starting transfers between devices, from_behind(): return lax.ppermute(value, axis, pairs)  9.93 us
    psum x1, blocking collectives, normed(): squares = lax.psum(jnp.sum(partial, axis=1), 'tp')  5.96 us
    unnamed x31, local copies, waits for them, and re-layouts  4.24 us
    convert_element_type x1, other arithmetic, normed(): return scaled.astype(jnp.bfloat16)  3.95 us
    pallas_call x1, Pallas kernels, close(): pl.pallas_call(close_kernel, in_specs=[vmem] * 4, out_specs=[vmem] * 2, o...  3.72 us
  transfers between devices with their start and end apart: 6, of which 5 were waited for; matrix products, arithmetic and copies ran while one was open for 11% of the time, Pallas kernels for 49%

profile of v1, /device:TPU:0, one launch (start us, length us, event | category | flops | bytes accessed | tf_op | source)
XLA Modules:
  0.0 100.2 jit_solution(7150544172164725099)
XLA Ops:
  0.6 0.0 copy-start.6
  0.6 0.0 copy-start.8
  0.7 4.1 %collective-permute-start = (bf16[3072,128]{1,0:T(8,128)(2,1)}, bf16[3072,128]{1,0:T(8,128)(2,1)S(1)}, u32[]{:S(2)}, u32[]{:S(2)}) collective-permute-start(bf16[3072,128]{1,0:T(8,128)(2,1)} %bitcast.58), channel_id=1, source_target_pairs={{0,8},{4,12},{8,0},{12,4},{1,9},{5,13},{9,1},{13,5},{2,10},{6,14},... | collective-permute-start | bytes 2359304 | tf_op jit(solution)/shard_map/ppermute | solution.py:19
  4.8 0.1 collective-permute-start.1
  4.9 2.3 %slice.15 = bf16[1,1024,2,128]{3,2,1,0:T(2,128)(2,1)} slice(bf16[1,1536,2,128]{3,2,1,0:T(2,128)(2,1)} %param.13), slice={[0:1], [0:1024], [0:2], [0:128]} | slice | bytes 1048576 | tf_op jit(solution)/shard_map/slice | solution.py:444
  7.1 2.8 %collective-permute-start.5 = (bf16[2048,128]{1,0:T(8,128)(2,1)}, bf16[2048,128]{1,0:T(8,128)(2,1)S(1)}, u32[]{:S(2)}, u32[]{:S(2)}) collective-permute-start(bf16[2048,128]{1,0:T(8,128)(2,1)} %bitcast.24), channel_id=1, source_target_pairs={{0,8},{4,12},{8,0},{12,4},{1,9},{5,13},{9,1},{13,5},{2,10},{6,14},... | collective-permute-start | bytes 1572872 | tf_op jit(solution)/shard_map/ppermute | solution.py:19
  9.9 1.8 %slice.14 = bf16[1,512,2,128]{3,2,1,0:T(2,128)(2,1)} slice(bf16[1,1536,2,128]{3,2,1,0:T(2,128)(2,1)} %param.13), slice={[0:1], [1024:1536], [0:2], [0:128]} | slice | bytes 524288 | tf_op jit(solution)/shard_map/slice | solution.py:445
  11.7 0.1 collective-permute-start.4
  11.9 1.8 %fusion = (bf16[1,256,2,128]{3,2,1,0:T(2,128)(2,1)}, bf16[1,256,2,128]{3,2,1,0:T(2,128)(2,1)S(1)}) fusion(bf16[1,512,2,128]{3,2,1,0:T(2,128)(2,1)} %param.16), kind=kLoop, calls=%fused_computation.11 | loop fusion | bytes 524288 | tf_op jit(solution)/shard_map/slice | solution.py:446
  13.7 2.8 %collective-permute-start.3 = (bf16[512,128]{1,0:T(8,128)(2,1)}, bf16[512,128]{1,0:T(8,128)(2,1)S(1)}, u32[]{:S(2)}, u32[]{:S(2)}) collective-permute-start(bf16[512,128]{1,0:T(8,128)(2,1)} %bitcast.22), channel_id=1, source_target_pairs={{0,8},{4,12},{8,0},{12,4},{1,9},{5,13},{9,1},{13,5},{2,10},{6,14},... | collective-permute-start | bytes 393224 | tf_op jit(solution)/shard_map/ppermute | solution.py:19
  16.5 0.0 copy-done.6
  16.5 0.1 copy.36
  16.6 0.0 copy-done.8
  16.6 0.0 copy-done.3
  16.6 0.1 copy.35
  16.7 0.0 copy-done.5
  16.8 0.5 copy.34
  17.4 0.0 copy-start.2
  17.4 0.1 maximum_bitcast_fusion.k_ref
  17.5 0.1 maximum_bitcast_fusion.1.v_ref
  17.5 1.4 %copy-done.2 = bf16[1,512,2048]{2,1,0:T(8,128)(2,1)S(1)} copy-done((bf16[1,512,2048]{2,1,0:T(8,128)(2,1)S(1)}, bf16[1,512,2048]{2,1,0:T(8,128)(2,1)}, u32[]{:S(2)}) %copy-start.2) | copy-done | bytes 2097176
  19.0 32.3 %prefill.1 = (f32[512,2048]{1,0:T(8,128)S(1)}, f32[512,128]{1,0:T(8,128)S(1)}) custom-call(bf16[16,512,128]{2,1,0:T(8,128)(2,1)S(1)} %bitcast.47, bf16[2,2048,128]{2,1,0:T(8,128)(2,1)S(1)} %maximum_bitcast_fusion.k_ref, bf16[2,2048,128]{2,1,0:T(8,128)(2,1)S(1)} %maximum_bitcast_fusion.1.v_ref, bf16[512,2048]{1,0:T(8,128)(2,1)S(1)} %bitcast.51), custom_call_target="tpu_custom_call" | custom-call | flops 17179869184 | bytes 16777216 | tf_op jit(solution)/shard_map/prefill/pallas_call | solution.py:55
  51.3 1.9 %copy-done = f32[512,2048]{1,0:T(8,128)} copy-done((f32[512,2048]{1,0:T(8,128)}, f32[512,2048]{1,0:T(8,128)S(1)}, u32[]{:S(2)}) %copy-start) | copy-done | bytes 4194328
  53.2 0.1 reduce_sum.9
  53.4 6.0 %psum.7 = f32[512]{0:T(512)S(1)} all-reduce(f32[512]{0:T(512)S(1)} %reduce_sum.9), channel_id=1, replica_groups=mesh['groups'=2,'pair'=4,'tp'=4] {'tp'}, use_global_device_ids=true, to_apply=%region_1.0 | all-reduce | flops 512 | bytes 4096 | tf_op jit(solution)/shard_map/psum | solution.py:414
  59.3 0.0 copy-done.11
  59.3 0.0 copy-start.7
  59.4 0.0 copy-start.12
  59.4 0.0 copy-start.9
  59.4 0.0 copy-start.10
  59.4 3.9 %multiply_convert_fusion = bf16[512,2048]{1,0:T(8,128)(2,1)} fusion(f32[512,2048]{1,0:T(8,128)} %copy-done, f32[2048]{0:T(1024)S(1)} %convert_element_type.7, f32[512]{0:T(512)S(1)} %add_rsqrt_fusion), kind=kLoop, calls=%fused_computation | loop fusion | flops 3145728 | bytes 6301696 | tf_op jit(solution)/shard_map/convert_element_type | solution.py:416
  63.4 0.1 copy.23
  63.4 0.0 copy-done.12
  63.4 0.1 broadcast_in_dim_tile.3
  63.5 0.1 copy.26.cur_ref
  63.7 7.5 %collective-permute-done.1.sk_ref = bf16[1024,128]{1,0:T(8,128)(2,1)S(1)} collective-permute-done((bf16[1024,128]{1,0:T(8,128)(2,1)}, bf16[1024,128]{1,0:T(8,128)(2,1)S(1)}, u32[]{:S(2)}, u32[]{:S(2)}) %collective-permute-start.1) | collective-permute-done | bytes 262176 | tf_op jit(solution)/shard_map/ppermute | solution.py:19
  71.1 0.0 collective-permute-start.2
  71.1 0.0 collective-permute-done.pk_ref
  71.1 11.6 %weigh.1 = (bf16[2,512,3584]{2,1,0:T(8,128)(2,1)S(1)}, bf16[2,512,512]{2,1,0:T(8,128)(2,1)S(1)}, f32[2,512,128]{2,1,0:T(8,128)S(1)}, f32[2,512,128]{2,1,0:T(8,128)S(1)}, bf16[4096,128]{1,0:T(8,128)(2,1)}) custom-call(bf16[2,512,128]{2,1,0:T(8,128)(2,1)S(1)} %bitcast.49, bf16[3072,128]{1,0:T(8,128)(2,1)S(1)} %collective-permute-done.pk_ref, ...), custom_call_target="tpu_custom_call" | custom-call | flops 2147483648 | bytes 16777216 | tf_op jit(solution)/shard_map/weigh/pallas_call | solution.py:139
  82.8 2.4 %collective-permute-done.5.v_ref = bf16[2048,128]{1,0:T(8,128)(2,1)S(1)} collective-permute-done((bf16[2048,128]{1,0:T(8,128)(2,1)}, bf16[2048,128]{1,0:T(8,128)(2,1)S(1)}, u32[]{:S(2)}, u32[]{:S(2)}) %collective-permute-start.5) | collective-permute-done | bytes 524320 | tf_op jit(solution)/shard_map/ppermute | solution.py:19
  85.2 2.4 %mix.1 = (f32[2,512,128]{2,1,0:T(8,128)S(1)}, bf16[4096,128]{1,0:T(8,128)(2,1)}) custom-call(bf16[2,512,3584]{2,1,0:T(8,128)(2,1)S(1)} %get-tuple-element.33.w_ref, bf16[2048,128]{1,0:T(8,128)(2,1)S(1)} %collective-permute-done.5.v_ref, f32[2,512,128]{2,1,0:T(8,128)S(1)} %get-tuple-element.34.own_ref), custom_call_target="tpu_custom_call" | custom-call | flops 1073741824 | bytes 8388608 | tf_op jit(solution)/shard_map/mix/pallas_call | solution.py:185
  87.6 3.2 %collective-permute-done.4.v_ref = bf16[1024,128]{1,0:T(8,128)(2,1)S(1)} collective-permute-done((bf16[1024,128]{1,0:T(8,128)(2,1)}, bf16[1024,128]{1,0:T(8,128)(2,1)S(1)}, u32[]{:S(2)}, u32[]{:S(2)}) %collective-permute-start.4) | collective-permute-done | bytes 262176 | tf_op jit(solution)/shard_map/ppermute | solution.py:19
  90.8 1.6 %mix_more.1 = (f32[2,512,128]{2,1,0:T(8,128)S(1)}, bf16[4096,128]{1,0:T(8,128)(2,1)}) custom-call(bf16[2,512,3584]{2,1,0:T(8,128)(2,1)S(1)} %get-tuple-element.33.w_ref, bf16[1024,128]{1,0:T(8,128)(2,1)S(1)} %collective-permute-done.4.v_ref, f32[2,512,128]{2,1,0:T(8,128)S(1)} %get-tuple-element.35.own_ref, ...), custom_call_target="tpu_custom_call", output_to_operand_aliasing={{1}: (3, {})} | custom-call | flops 536870912 | bytes 6291456 | tf_op jit(solution)/shard_map/mix_more/pallas_call | solution.py:218
  92.4 1.2 %collective-permute-done.3.v_ref.s_ref = bf16[512,128]{1,0:T(8,128)(2,1)S(1)} collective-permute-done((bf16[512,128]{1,0:T(8,128)(2,1)}, bf16[512,128]{1,0:T(8,128)(2,1)S(1)}, u32[]{:S(2)}, u32[]{:S(2)}) %collective-permute-start.3) | collective-permute-done | bytes 131104 | tf_op jit(solution)/shard_map/ppermute | solution.py:19
  93.6 0.8 gather.1.part_ref
  94.4 1.2 %collective-permute-done.2.v_ref.t_ref = bf16[512,128]{1,0:T(8,128)(2,1)S(1)} collective-permute-done((bf16[512,128]{1,0:T(8,128)(2,1)S(1)}, bf16[512,128]{1,0:T(8,128)(2,1)S(1)}, u32[]{:S(2)}, u32[]{:S(2)}) %collective-permute-start.2) | collective-permute-done | bytes 131104 | tf_op jit(solution)/shard_map/ppermute | solution.py:19
  95.6 3.7 %close.1 = (f32[64,2048]{1,0:T(8,128)S(1)}, f32[8,128]{1,0:T(8,128)S(1)}) custom-call(bf16[2,512,512]{2,1,0:T(8,128)(2,1)S(1)} %get-tuple-element.32.w_ref, bf16[512,128]{1,0:T(8,128)(2,1)S(1)} %collective-permute-done.2.v_ref.t_ref, f32[64,2048]{1,0:T(8,128)S(1)} %gather.1.part_ref, f32[2,512,128]{2,1,0:T(8,128)S(1)} %get-tuple-element.38.inv_ref), custom_call_target="tpu_custom_call" | custom-call | flops 268435456 | bytes 4194304 | tf_op jit(solution)/shard_map/close/pallas_call | solution.py:333
  99.3 0.9 write.1
  (17 shorter events, 0.1 us)
Async XLA Ops:
  0.6 15.8 %copy-start.6 = (bf16[1,1536,2,128]{3,2,1,0:T(2,128)(2,1)S(1)}, bf16[1,1536,2,128]{3,2,1,0:T(2,128)(2,1)}, u32[]{:S(2)}) copy-start(bf16[1,1536,2,128]{3,2,1,0:T(2,128)(2,1)} %param.12) | copy-start | bytes 2359300
  0.6 15.9 %copy-start.8 = (bf16[1,512,2,128]{3,2,1,0:T(2,128)(2,1)S(1)}, bf16[1,512,2,128]{3,2,1,0:T(2,128)(2,1)}, u32[]{:S(2)}) copy-start(bf16[1,512,2,128]{3,2,1,0:T(2,128)(2,1)} %param.15) | copy-start | bytes 786436
  0.7 70.5 %collective-permute-start = (bf16[3072,128]{1,0:T(8,128)(2,1)}, bf16[3072,128]{1,0:T(8,128)(2,1)S(1)}, u32[]{:S(2)}, u32[]{:S(2)}) collective-permute-start(bf16[3072,128]{1,0:T(8,128)(2,1)} %bitcast.58), channel_id=1, source_target_pairs={{0,8},{4,12},{8,0},{12,4},{1,9},{5,13},{9,1},{13,5},{2,10},{6,14},... | collective-permute-start | bytes 2359304 | tf_op jit(solution)/shard_map/ppermute | solution.py:19
  4.8 11.8 %copy-start.3 = (bf16[1,1536,2,128]{3,2,1,0:T(2,128)(2,1)S(1)}, bf16[1,1536,2,128]{3,2,1,0:T(2,128)(2,1)}, u32[]{:S(2)}) copy-start(bf16[1,1536,2,128]{3,2,1,0:T(2,128)(2,1)} %param.13) | copy-start | bytes 2359300
  4.8 66.3 %collective-permute-start.1 = (bf16[1024,128]{1,0:T(8,128)(2,1)}, bf16[1024,128]{1,0:T(8,128)(2,1)S(1)}, u32[]{:S(2)}, u32[]{:S(2)}) collective-permute-start(bf16[1024,128]{1,0:T(8,128)(2,1)} %bitcast.60), channel_id=1, source_target_pairs={{0,8},{4,12},{8,0},{12,4},{1,9},{5,13},{9,1},{13,5},{2,10},{6,14},... | collective-permute-start | bytes 786440 | tf_op jit(solution)/shard_map/ppermute | solution.py:19
  7.1 78.1 %collective-permute-start.5 = (bf16[2048,128]{1,0:T(8,128)(2,1)}, bf16[2048,128]{1,0:T(8,128)(2,1)S(1)}, u32[]{:S(2)}, u32[]{:S(2)}) collective-permute-start(bf16[2048,128]{1,0:T(8,128)(2,1)} %bitcast.24), channel_id=1, source_target_pairs={{0,8},{4,12},{8,0},{12,4},{1,9},{5,13},{9,1},{13,5},{2,10},{6,14},... | collective-permute-start | bytes 1572872 | tf_op jit(solution)/shard_map/ppermute | solution.py:19
  11.7 5.0 %copy-start.5 = (bf16[1,512,2,128]{3,2,1,0:T(2,128)(2,1)S(1)}, bf16[1,512,2,128]{3,2,1,0:T(2,128)(2,1)}, u32[]{:S(2)}) copy-start(bf16[1,512,2,128]{3,2,1,0:T(2,128)(2,1)} %param.16) | copy-start | bytes 786436
  11.7 79.1 %collective-permute-start.4 = (bf16[1024,128]{1,0:T(8,128)(2,1)}, bf16[1024,128]{1,0:T(8,128)(2,1)S(1)}, u32[]{:S(2)}, u32[]{:S(2)}) collective-permute-start(bf16[1024,128]{1,0:T(8,128)(2,1)} %bitcast.23), channel_id=1, source_target_pairs={{0,8},{4,12},{8,0},{12,4},{1,9},{5,13},{9,1},{13,5},{2,10},{6,14},... | collective-permute-start | bytes 786440 | tf_op jit(solution)/shard_map/ppermute | solution.py:19
  13.7 3.1 %copy-start.4 = (bf16[1,512,16,128]{3,2,1,0:T(8,128)(2,1)S(1)}, bf16[1,512,16,128]{3,2,1,0:T(8,128)(2,1)}, u32[]{:S(2)}) copy-start(bf16[1,512,16,128]{3,2,1,0:T(8,128)(2,1)} %param.14) | copy-start | bytes 6291460
  13.7 79.9 %collective-permute-start.3 = (bf16[512,128]{1,0:T(8,128)(2,1)}, bf16[512,128]{1,0:T(8,128)(2,1)S(1)}, u32[]{:S(2)}, u32[]{:S(2)}) collective-permute-start(bf16[512,128]{1,0:T(8,128)(2,1)} %bitcast.22), channel_id=1, source_target_pairs={{0,8},{4,12},{8,0},{12,4},{1,9},{5,13},{9,1},{13,5},{2,10},{6,14},... | collective-permute-start | bytes 393224 | tf_op jit(solution)/shard_map/ppermute | solution.py:19
  17.4 1.6 %copy-start.2 = (bf16[1,512,2048]{2,1,0:T(8,128)(2,1)S(1)}, bf16[1,512,2048]{2,1,0:T(8,128)(2,1)}, u32[]{:S(2)}) copy-start(bf16[1,512,2048]{2,1,0:T(8,128)(2,1)} %param.17) | copy-start | bytes 6291460
  19.0 40.4 %copy-start.11 = (bf16[2048]{0:T(1024)(128)(2,1)S(1)}, bf16[2048]{0:T(1024)(128)(2,1)}, u32[]{:S(2)}) copy-start(bf16[2048]{0:T(1024)(128)(2,1)} %param.23) | copy-start | bytes 12292
  51.3 1.9 %copy-start = (f32[512,2048]{1,0:T(8,128)}, f32[512,2048]{1,0:T(8,128)S(1)}, u32[]{:S(2)}) copy-start(f32[512,2048]{1,0:T(8,128)S(1)} %get-tuple-element.24) | copy-start | bytes 12582916
  59.3 4.0 %copy-start.7 = (bf16[1,2,32,16,128]{4,3,2,1,0:T(8,128)(2,1)S(1)}, bf16[1,2,32,16,128]{4,3,2,1,0:T(8,128)(2,1)}, u32[]{:S(2)}) copy-start(bf16[1,2,32,16,128]{4,3,2,1,0:T(8,128)(2,1)} %param.18) | copy-start | bytes 786436
  59.4 4.1 %copy-start.12 = (s32[1,32]{1,0:T(1,128)S(1)}, s32[1,32]{1,0:T(1,128)}, u32[]{:S(2)}) copy-start(s32[1,32]{1,0:T(1,128)} %param.22) | copy-start | bytes 388
  59.4 4.2 %copy-start.9 = (bf16[1,2,32,2,128]{4,3,2,1,0:T(2,128)(2,1)S(1)}, bf16[1,2,32,2,128]{4,3,2,1,0:T(2,128)(2,1)}, u32[]{:S(2)}) copy-start(bf16[1,2,32,2,128]{4,3,2,1,0:T(2,128)(2,1)} %param.20) | copy-start | bytes 98308
  59.4 4.1 %copy-start.10 = (bf16[1,2,32,2,128]{4,3,2,1,0:T(2,128)(2,1)S(1)}, bf16[1,2,32,2,128]{4,3,2,1,0:T(2,128)(2,1)}, u32[]{:S(2)}) copy-start(bf16[1,2,32,2,128]{4,3,2,1,0:T(2,128)(2,1)} %param.19) | copy-start | bytes 98308
  71.1 24.4 %collective-permute-start.2 = (bf16[512,128]{1,0:T(8,128)(2,1)S(1)}, bf16[512,128]{1,0:T(8,128)(2,1)S(1)}, u32[]{:S(2)}, u32[]{:S(2)}) collective-permute-start(bf16[512,128]{1,0:T(8,128)(2,1)S(1)} %bitcast.61), channel_id=1, source_target_pairs={{0,8},{4,12},{8,0},{12,4},{1,9},{5,13},{9,1},{13,5},{2,10},{6,14},... | collective-permute-start | bytes 393224 | tf_op jit(solution)/shard_map/ppermute | solution.py:19
  90.8 2.8 %copy-start.1 = (bf16[1,2,32,2048]{3,2,1,0:T(8,128)(2,1)S(1)}, bf16[1,2,32,2048]{3,2,1,0:T(8,128)(2,1)}, u32[]{:S(2)}) copy-start(bf16[1,2,32,2048]{3,2,1,0:T(8,128)(2,1)} %param.21) | copy-start | bytes 786436
